TPU v7x, 32 devices: a whole 2x2x4 slice. The times are simulated.
32 devices in a mesh: group: 1, ctx: 32 (over z, y, x, core).
Axes of the slice: x: 2, y: 2, z: 4, core: 2. Of those that a mesh axis runs over, the one named last changes fastest.
Arguments:
- queries: bfloat16 [2, 64, 128], P('group'), may hold values from -80 to 80
- key_cache: bfloat16 [2, 4096, 512], P('group', 'ctx'), may hold values from -4 to 4
- value_cache: bfloat16 [2, 4096, 512], P('group', 'ctx'), may hold values from -6 to 6
- out_weight: bfloat16 [8192, 4096], P('ctx'), may hold values from -0.125 to 0.125
- hidden_in: bfloat16 [2, 4096], P('group'), may hold values from -45 to 45
- norm_gain: float32 [4096], replicated, may hold values from 0.25 to 1.75
- gate_weight: bfloat16 [32, 4096, 192], P('ctx'), may hold values from -0.09375 to 0.09375
- up_weight: bfloat16 [32, 4096, 192], P('ctx'), may hold values from -0.09375 to 0.09375
- down_weight: bfloat16 [32, 192, 4096], P('ctx'), may hold values from -0.15625 to 0.15625
- routes: int32 [2, 4], P('group'), may hold values from 0 to 3, all different within a row; in each aligned block of 2 rows (0 to 1, 2 to 3, ...) at most 2 rows name the same one
- route_weight: float32 [2, 4], P('group'), may hold values from 0.1 to 1
Outputs:
- mixed: float32 [2, 4096], P('group', 'ctx')
Inputs may be any that keep to these rules, and one draw needn't show every extreme that they name: `routes`: each row names 4 different experts; no expert is named by more than 2 rows, a bound that some block reaches.
All inputs are finite; a program needn't handle non-finite values.
Results may differ from a plain program's by a relative error of at most 0.0035.
Values may be sent and summed in bfloat16 or wider, within the bound.
No kernel may reach another device: no remote copies, remote signals or barrier semaphores. Data moves between devices by JAX's collectives and lax.ppermute only.
A program may use at most 64 MiB of HBM per device.

v0:
```python
import jax
import jax.numpy as jnp
from jax import lax
from jax.sharding import PartitionSpec as P

QUARTERS = 8
eps = 1e-06


def slot_numbers(routes, expert_count):
    flat_routes = routes.reshape(-1)
    onehot = (flat_routes[:, None] == jnp.arange(expert_count, dtype=jnp.int32)[None, :]).astype(
        jnp.int32
    )
    before = jnp.cumsum(onehot, axis=0) - onehot
    return jnp.sum(before * onehot, axis=1)


def body(
    queries,
    key_cache,
    value_cache,
    out_weight,
    hidden_in,
    norm_gain,
    gate_weight,
    up_weight,
    down_weight,
    routes,
    route_weight,
):
    devices = lax.axis_size("ctx")
    my_index = lax.axis_index("ctx")
    seq_count, head_count, head_dim = queries.shape
    kv_heads = key_cache.shape[2] // head_dim
    group_size = head_count // kv_heads
    model_width = hidden_in.shape[1]
    local_len = key_cache.shape[1]
    query_view = queries.reshape(seq_count, kv_heads, group_size, head_dim)
    key_view = key_cache.reshape(seq_count, local_len, kv_heads, head_dim)
    value_view = value_cache.reshape(seq_count, local_len, kv_heads, head_dim)
    scores = jnp.einsum(
        "sgjd,scgd->sgjc", query_view, key_view, preferred_element_type=jnp.float32
    ) * head_dim ** (-0.5)
    row_peak = lax.pmax(jnp.max(scores, axis=-1), "ctx")
    numer = jnp.exp(scores - row_peak[..., None])
    denom_part = jnp.sum(numer, axis=-1)
    partial_value = jnp.einsum(
        "sgjc,scgd->sgjd",
        numer.astype(jnp.bfloat16),
        value_view,
        preferred_element_type=jnp.float32,
    )
    partial_value = partial_value.reshape(seq_count, head_count * head_dim)
    feat_dev = head_count * head_dim // devices
    feat_start = my_index * feat_dev
    summed, denoms = lax.psum((partial_value, denom_part), "ctx")
    attn_mine = lax.dynamic_slice_in_dim(summed, feat_start, feat_dev, 1)
    spread_denoms = jnp.repeat(denoms.reshape(seq_count, head_count), head_dim, axis=1)
    mine_denoms = lax.dynamic_slice_in_dim(spread_denoms, feat_start, feat_dev, 1)
    attended = (attn_mine / mine_denoms).astype(jnp.bfloat16)
    proj_part = jnp.dot(attended, out_weight, preferred_element_type=jnp.float32)
    col_dev = model_width // devices
    col_start = my_index * col_dev
    projected = lax.psum(proj_part, "ctx")
    resid = hidden_in.astype(jnp.float32) + projected
    inverse_rms = lax.rsqrt(jnp.mean(resid * resid, axis=-1, keepdims=True) + eps)
    normed = (resid * inverse_rms * norm_gain).astype(jnp.bfloat16)
    resid_mine = lax.dynamic_slice_in_dim(resid, col_start, col_dev, 1)
    expert_count = devices // QUARTERS
    top_count = routes.shape[1]
    capacity = min(2 * seq_count * top_count // expert_count, seq_count)
    expert = my_index // QUARTERS
    slot_index = slot_numbers(routes, expert_count)
    flat_routes = routes.reshape(-1)
    token_of = jnp.arange(seq_count * top_count, dtype=jnp.int32) // top_count
    matches = (
        (flat_routes[None, :] == expert)
        & (slot_index[None, :] == jnp.arange(capacity, dtype=jnp.int32)[:, None])
    ).astype(jnp.float32)
    owners = (token_of[:, None] == jnp.arange(seq_count, dtype=jnp.int32)[None, :]).astype(
        jnp.float32
    )
    select = jnp.dot(matches, owners, precision=lax.Precision.HIGHEST)
    slot_weight = jnp.dot(matches, route_weight.reshape(-1), precision=lax.Precision.HIGHEST)
    picked_rows = jnp.dot(
        select.astype(jnp.bfloat16), normed, preferred_element_type=jnp.float32
    ).astype(jnp.bfloat16)
    gate_act = jnp.dot(picked_rows, gate_weight[0], preferred_element_type=jnp.float32)
    up_act = jnp.dot(picked_rows, up_weight[0], preferred_element_type=jnp.float32)
    hidden = (jax.nn.silu(gate_act) * up_act).astype(jnp.bfloat16)
    expert_out = (
        jnp.dot(hidden, down_weight[0], preferred_element_type=jnp.float32) * slot_weight[:, None]
    )
    received = lax.all_to_all(
        expert_out.astype(jnp.bfloat16), "ctx", split_axis=1, concat_axis=0, tiled=True
    ).astype(expert_out.dtype)
    quarter_ids = jnp.arange(QUARTERS, dtype=jnp.int32)[None, None, :]
    shard_rows = (routes[:, :, None] * QUARTERS + quarter_ids) * capacity + slot_index.reshape(
        seq_count, top_count
    )[:, :, None]
    moe_mine = jnp.sum(received[shard_rows], axis=(1, 2))
    return resid_mine + moe_mine


def solution(mesh):
    in_specs = (
        P("group", None, None),
        P("group", "ctx", None),
        P("group", "ctx", None),
        P("ctx", None),
        P("group", None),
        P(),
        P("ctx", None, None),
        P("ctx", None, None),
        P("ctx", None, None),
        P("group", None),
        P("group", None),
    )
    out_specs = P("group", "ctx")
    return jax.shard_map(body, mesh=mesh, in_specs=in_specs, out_specs=out_specs, check_vma=False)
```

profile of v0, /device:TPU:0, one launch (start us, length us, event | category | flops | bytes accessed | tf_op | source)
XLA Modules:
  0.0 239.1 jit_solution(7500703949883063939)
XLA Ops:
  6.5 1.4 fusion.41
  8.0 42.0 %pmax.7 = f32[2,4,16]{2,1,0:T(4,128)S(1)} all-reduce(f32[2,4,16]{2,1,0:T(4,128)S(1)} %get-tuple-element.7), channel_id=1, replica_groups=mesh['group'=1,'ctx'=32] {'ctx'}, use_global_device_ids=true, to_apply=%region_1.0 | all-reduce | flops 128 | bytes 1024 | tf_op jit(solution)/shard_map/pmax | solution.py:45
  50.0 1.2 fusion.17
  51.2 0.7 copy.38
  51.9 0.8 broadcast_in_dim_reshape.2
  52.7 0.7 broadcast_multiply_fusion
  53.3 0.2 fusion.22
  53.6 0.8 reshape.100
  54.3 0.2 reduce_window_sum.11
  54.7 40.0 %psum.22 = f32[2,64]{1,0:T(2,128)S(1)} all-reduce(f32[2,64]{1,0:T(2,128)S(1)} %reshape.87), channel_id=1, replica_groups=mesh['group'=1,'ctx'=32] {'ctx'}, use_global_device_ids=true, to_apply=%region_4.0 | all-reduce | flops 128 | bytes 1024 | tf_op jit(solution)/shard_map/psum | solution.py:57
  94.8 0.2 convolution_convert_fusion.1
  95.1 0.1 convolution_bitcast_fusion
  95.2 0.1 reshape.93
  95.3 76.0 %all-reduce.2.cloned.1.call-done = f32[2,8192]{1,0:T(2,128)} async-done(((f32[2,8192]{1,0:T(2,128)}), f32[2,8192]{1,0:T(2,128)}) %all-reduce.2.cloned.1.call-update) | async-done | bytes 65552 | tf_op jit(solution)/shard_map/psum | solution.py:57
  171.4 1.1 fusion.32
  172.4 41.0 %psum.23 = f32[2,4096]{1,0:T(2,128)S(1)} all-reduce(f32[2,4096]{1,0:T(2,128)S(1)} %fusion.32), channel_id=1, replica_groups=mesh['group'=1,'ctx'=32] {'ctx'}, use_global_device_ids=true, to_apply=%region_5.0 | all-reduce | flops 8192 | bytes 65536 | tf_op jit(solution)/shard_map/psum | solution.py:65
  213.5 0.1 multiply_reduce_fusion
  213.6 0.2 convolution_convert_fusion
  213.8 1.9 fusion.4
  215.8 3.7 %fusion.6 = bf16[2,32,128]{2,0,1:T(2,128)(2,1)} fusion(bf16[1,192,4096]{2,1,0:T(8,128)(2,1)} %param.19, bf16[2,4096]{1,0:T(2,128)(2,1)S(1)} %convolution_convert_fusion, bf16[1,4096,192]{1,2,0:T(8,128)(2,1)} %param.18, f32[2]{0:T(128)S(1)} %convolution_bitcast_fusion, f32[2,192]{1,0:T(2,128)S(1)} %fusion.4), kind=kOutput, calls=%fused_computation.10 | convolution fusion | flops 6310144 | bytes 3180040 | tf_op jit(solution)/shard_map/dot_general | solution.py:93
  219.5 4.4 %all-to-all-start = ((bf16[2,32,128]{2,0,1:T(2,128)(2,1)}), bf16[2,32,128]{2,0,1:T(2,128)(2,1)S(1)}, u32[]{:S(2)}, u32[]{:S(2)}) async-start(bf16[2,32,128]{2,0,1:T(2,128)(2,1)} %fusion.6), calls=%async_computation | async-start | bytes 32768 | tf_op jit(solution)/shard_map/all_to_all | solution.py:95
  223.9 7.2 %all-to-all-done = bf16[2,32,128]{2,0,1:T(2,128)(2,1)S(1)} async-done(((bf16[2,32,128]{2,0,1:T(2,128)(2,1)}), bf16[2,32,128]{2,0,1:T(2,128)(2,1)S(1)}, u32[]{:S(2)}, u32[]{:S(2)}) %all-to-all-start) | async-done | bytes 16416 | tf_op jit(solution)/shard_map/all_to_all | solution.py:95
  231.1 0.6 gather_fusion
  231.7 0.6 dynamic-slice_add_fusion
  (21 shorter events, 0.5 us)
Async XLA Ops:
  6.5 164.8 %copy-start = (bf16[256,4096]{1,0:T(8,128)(2,1)S(1)}, bf16[256,4096]{1,0:T(8,128)(2,1)}, u32[]{:S(2)}) copy-start(bf16[256,4096]{1,0:T(8,128)(2,1)} %param.14) | copy-start | bytes 6291460
  6.5 164.8 %all-reduce.2.cloned.1.call-start = ((), (), s32[]{:S(2)}) async-start(), calls=%async_computation.1 | async-start | bytes 131072 | tf_op jit(solution)/shard_map/psum | solution.py:57
  50.0 163.5 %copy-start.1 = (bf16[2,4096]{1,0:T(2,128)(2,1)S(1)}, bf16[2,4096]{1,0:T(2,128)(2,1)}, u32[]{:S(2)}) copy-start(bf16[2,4096]{1,0:T(2,128)(2,1)} %param.15) | copy-start | bytes 49156
  50.0 163.6 %copy-start.2 = (f32[4096]{0:T(1024)S(1)}, f32[4096]{0:T(1024)}, u32[]{:S(2)}) copy-start(f32[4096]{0:T(1024)} %param.16) | copy-start | bytes 49156
  219.5 11.6 %all-to-all-start = ((bf16[2,32,128]{2,0,1:T(2,128)(2,1)}), bf16[2,32,128]{2,0,1:T(2,128)(2,1)S(1)}, u32[]{:S(2)}, u32[]{:S(2)}) async-start(bf16[2,32,128]{2,0,1:T(2,128)(2,1)} %fusion.6), calls=%async_computation | async-start | bytes 32768 | tf_op jit(solution)/shard_map/all_to_all | solution.py:95
Sparse Core Ops, SparseCore 0:
  52.0 119.3 all-reduce.1
where the time goes:
time: 240 us; the launch traced here: 239 us
  blocking collectives  123 us (51%)
  waiting for transfers between devices  83.2 us (35%)
  between operations  13.5 us (6%)
  matrix products  9.84 us (4%)
  starting transfers between devices  4.4 us (2%)
  local copies, waits for them, and re-layouts  3.2 us (1%)
    psum x1, waiting for transfers between devices, body(): summed, denoms = lax.psum((partial_value, denom_part), 'ctx')  76 us
    pmax x1, blocking collectives, body(): row_peak = lax.pmax(jnp.max(scores, axis=-1), 'ctx')  42 us
    psum x1, blocking collectives, body(): projected = lax.psum(proj_part, 'ctx')  41 us
    psum x1, blocking collectives, body(): summed, denoms = lax.psum((partial_value, denom_part), 'ctx')  40 us
    all_to_all x1, waiting for transfers between devices, body(): lax.all_to_all(expert_out.astype(jnp.bfloat16), 'ctx', split_axis=1, conc...  7.16 us
  transfers between devices with their start and end apart: 2, of which 2 were waited for; matrix products, arithmetic and copies ran while one was open for 1% of the time, Pallas kernels for 0%

commit v1 on v0

--- a/solution.py
+++ b/solution.py
@@ -2,6 +2,7 @@
 import jax.numpy as jnp
 from jax import lax
 from jax.sharding import PartitionSpec as P
+from jax.lax import all_gather
 
 QUARTERS = 8
 eps = 1e-06
@@ -62,7 +63,7 @@
     proj_part = jnp.dot(attended, out_weight, preferred_element_type=jnp.float32)
     col_dev = model_width // devices
     col_start = my_index * col_dev
-    projected = lax.psum(proj_part, "ctx")
+    projected = all_gather(proj_part, "ctx").sum(axis=0)
     resid = hidden_in.astype(jnp.float32) + projected
     inverse_rms = lax.rsqrt(jnp.mean(resid * resid, axis=-1, keepdims=True) + eps)
     normed = (resid * inverse_rms * norm_gain).astype(jnp.bfloat16)

time: 240 us -> 256 us (1.067)
  waiting for transfers between devices: 83.2 us -> 141 us
  blocking collectives: 123 us -> 82.1 us
    all_gather x0 -> x1, waiting for transfers between devices: none -> 55 us  [body(): projected = all_gather(proj_part, 'ctx').sum(axis=0)]
    psum x1 -> x0, blocking collectives: 41 us -> none  [body(): projected = lax.psum(proj_part, 'ctx')]
    psum x1, waiting for transfers between devices: 76 us -> 78.8 us  [body(): summed, denoms = lax.psum((partial_value, denom_part), 'ctx')]
  transfers between devices with their start and end apart: 2 -> 3, of which waited for: 2 -> 3; matrix products, arithmetic and copies ran while one was open for 1% -> 1% of each run, Pallas kernels for 0% -> 0%
where the time goes in v1:
time: 256 us; the launch traced here: 255 us
  waiting for transfers between devices  141 us (55%)
  blocking collectives  82.1 us (32%)
  between operations  13.5 us (5%)
  matrix products  10.4 us (4%)
  starting transfers between devices  3.62 us (1%)
  other arithmetic  2.79 us (1%)
    psum x1, waiting for transfers between devices, body(): summed, denoms = lax.psum((partial_value, denom_part), 'ctx')  78.8 us
    all_gather x1, waiting for transfers between devices, body(): projected = all_gather(proj_part, 'ctx').sum(axis=0)  55 us
    pmax x1, blocking collectives, body(): row_peak = lax.pmax(jnp.max(scores, axis=-1), 'ctx')  42 us
    psum x1, blocking collectives, body(): summed, denoms = lax.psum((partial_value, denom_part), 'ctx')  40.1 us
    all_to_all x1, waiting for transfers between devices, body(): lax.all_to_all(expert_out.astype(jnp.bfloat16), 'ctx', split_axis=1, conc...  7.16 us
  transfers between devices with their start and end apart: 3, of which 3 were waited for; matrix products, arithmetic and copies ran while one was open for 1% of the time, Pallas kernels for 0%

profile of v1, /device:TPU:0, one launch (start us, length us, event | category | flops | bytes accessed | tf_op | source)
XLA Modules:
  0.0 255.4 jit_solution(15150535901822587929)
XLA Ops:
  6.5 1.4 fusion.40
  8.0 42.0 %pmax.7 = f32[2,4,16]{2,1,0:T(4,128)S(1)} all-reduce(f32[2,4,16]{2,1,0:T(4,128)S(1)} %get-tuple-element.7), channel_id=1, replica_groups=mesh['group'=1,'ctx'=32] {'ctx'}, use_global_device_ids=true, to_apply=%region_1.0 | all-reduce | flops 128 | bytes 1024 | tf_op jit(solution)/shard_map/pmax | solution.py:46
  50.0 1.2 fusion.17
  51.2 0.7 copy.38
  51.9 0.2 fusion.22
  52.1 0.1 reshape.87
  52.2 40.1 %psum.15 = f32[2,64]{1,0:T(2,128)S(1)} all-reduce(f32[2,64]{1,0:T(2,128)S(1)} %reshape.87), channel_id=1, replica_groups=mesh['group'=1,'ctx'=32] {'ctx'}, use_global_device_ids=true, to_apply=%region_4.0 | all-reduce | flops 128 | bytes 1024 | tf_op jit(solution)/shard_map/psum | solution.py:58
  92.5 78.8 %all-reduce.2.cloned.1.call-done = f32[2,8192]{1,0:T(2,128)} async-done(((f32[2,8192]{1,0:T(2,128)}), f32[2,8192]{1,0:T(2,128)}) %all-reduce.2.cloned.1.call-update) | async-done | bytes 65552 | tf_op jit(solution)/shard_map/psum | solution.py:58
  171.3 1.7 convolution_bitcast_fusion
  173.1 0.2 reduce_window_sum.11
  173.4 0.1 add.93
  173.6 0.1 reshape.93
  173.7 0.1 convolution_bitcast_fusion.1
  173.8 0.2 convolution_convert_fusion.1
  174.0 55.0 %all-gather.4.cloned.1.call-done = f32[32,2,4096]{2,1,0:T(2,128)} async-done(((f32[1,2,4096]{2,1,0:T(2,128)}), f32[32,2,4096]{2,1,0:T(2,128)}) %all-gather.4.cloned.1.call-update) | async-done | bytes 1048592 | tf_op jit(solution)/shard_map/all_gather | solution.py:66
  229.0 1.5 reduce_sum.46
  230.6 0.1 multiply_reduce_fusion
  230.8 0.2 convolution_convert_fusion
  231.0 1.9 fusion.4
  232.9 3.7 %fusion.6 = bf16[2,32,128]{2,0,1:T(2,128)(2,1)} fusion(bf16[1,192,4096]{2,1,0:T(8,128)(2,1)} %param.19, bf16[2,4096]{1,0:T(2,128)(2,1)S(1)} %convolution_convert_fusion, bf16[1,4096,192]{1,2,0:T(8,128)(2,1)} %param.18, f32[2]{0:T(128)S(1)} %convolution_bitcast_fusion.1, f32[2,192]{1,0:T(2,128)S(1)} %fusion.4), kind=kOutput, calls=%fused_computation.11 | convolution fusion | flops 6310144 | bytes 3180040 | tf_op jit(solution)/shard_map/dot_general | solution.py:94
  236.6 3.6 %all-to-all-start = ((bf16[2,32,128]{2,0,1:T(2,128)(2,1)}), bf16[2,32,128]{2,0,1:T(2,128)(2,1)S(1)}, u32[]{:S(2)}, u32[]{:S(2)}) async-start(bf16[2,32,128]{2,0,1:T(2,128)(2,1)} %fusion.6), calls=%async_computation | async-start | bytes 32768 | tf_op jit(solution)/shard_map/all_to_all | solution.py:96
  240.2 7.2 %all-to-all-done = bf16[2,32,128]{2,0,1:T(2,128)(2,1)S(1)} async-done(((bf16[2,32,128]{2,0,1:T(2,128)(2,1)}), bf16[2,32,128]{2,0,1:T(2,128)(2,1)S(1)}, u32[]{:S(2)}, u32[]{:S(2)}) %all-to-all-start) | async-done | bytes 16416 | tf_op jit(solution)/shard_map/all_to_all | solution.py:96
  247.4 0.6 gather_fusion
  248.0 0.6 dynamic-slice_add_fusion
  (28 shorter events, 0.6 us)
Async XLA Ops:
  6.5 164.8 %copy-start = (bf16[256,4096]{1,0:T(8,128)(2,1)S(1)}, bf16[256,4096]{1,0:T(8,128)(2,1)}, u32[]{:S(2)}) copy-start(bf16[256,4096]{1,0:T(8,128)(2,1)} %param.14) | copy-start | bytes 6291460
  6.5 164.8 %all-reduce.2.cloned.1.call-start = ((), (), s32[]{:S(2)}) async-start(), calls=%async_computation.1 | async-start | bytes 131072 | tf_op jit(solution)/shard_map/psum | solution.py:58
  8.0 165.1 %copy-start.2 = (s32[2,4]{1,0:T(2,128)S(1)}, s32[2,4]{1,0:T(2,128)}, u32[]{:S(2)}) copy-start(s32[2,4]{1,0:T(2,128)} %param.20) | copy-start | bytes 100
  8.0 165.3 %copy-start.4 = (f32[2,4]{1,0:T(2,128)S(1)}, f32[2,4]{1,0:T(2,128)}, u32[]{:S(2)}) copy-start(f32[2,4]{1,0:T(2,128)} %param.21) | copy-start | bytes 100
  51.9 177.1 %all-gather.4.cloned.1.call-start = ((), (), s32[]{:S(2)}) async-start(), calls=%async_computation.2 | async-start | bytes 1081344 | tf_op jit(solution)/shard_map/all_gather | solution.py:66
  171.3 59.3 %copy-start.1 = (bf16[2,4096]{1,0:T(2,128)(2,1)S(1)}, bf16[2,4096]{1,0:T(2,128)(2,1)}, u32[]{:S(2)}) copy-start(bf16[2,4096]{1,0:T(2,128)(2,1)} %param.15) | copy-start | bytes 49156
  171.3 59.4 %copy-start.3 = (f32[4096]{0:T(1024)S(1)}, f32[4096]{0:T(1024)}, u32[]{:S(2)}) copy-start(f32[4096]{0:T(1024)} %param.16) | copy-start | bytes 49156
  236.6 10.8 %all-to-all-start = ((bf16[2,32,128]{2,0,1:T(2,128)(2,1)}), bf16[2,32,128]{2,0,1:T(2,128)(2,1)S(1)}, u32[]{:S(2)}, u32[]{:S(2)}) async-start(bf16[2,32,128]{2,0,1:T(2,128)(2,1)} %fusion.6), calls=%async_computation | async-start | bytes 32768 | tf_op jit(solution)/shard_map/all_to_all | solution.py:96
Sparse Core Ops, SparseCore 0:
  52.0 119.2 all-reduce.1
  174.2 54.8 all-gather.3
